TPU v7x, 32 devices: a whole 2x2x4 slice. The times are simulated.
32 devices in a mesh: rows: 8 (over z, y), cols: 4 (over x, core).
Axes of the slice: x: 2, y: 2, z: 4, core: 2. Of those that a mesh axis runs over, the one named last changes fastest.
Arguments:
- weight_up: bfloat16 [12288, 49152], P('rows', 'cols'), may hold values from -0.078125 to 0.078125
- low_up: bfloat16 [12288, 64], P('rows'), may hold values from -0.0546875 to 0.0546875
- high_up: bfloat16 [64, 49152], P(None, 'cols'), may hold values from -0.75 to 0.75
- norm_train: float32 [12288], P(('rows', 'cols')), may hold values from 0.25 to 1.75
- norm_step: float32 [12288], P(('rows', 'cols')), may hold values from -0.3 to 0.3
Outputs:
- serve_up: bfloat16 [12288, 49152], P(None, ('cols', 'rows'))
- scale_up: float32 [49152], P(('cols', 'rows'))
- serve_norm: bfloat16 [12288], replicated
All inputs are finite; a program needn't handle non-finite values.
Results may differ from a plain program's by a relative error of at most 0.0004.
Values may be sent and summed in bfloat16 or wider, within the bound.
No kernel may reach another device: no remote copies, remote signals or barrier semaphores. Data moves between devices by JAX's collectives and lax.ppermute only.
A program may use at most 256 MiB of HBM per device.

v0:
```python
import jax
import jax.numpy as jnp
from jax import lax
from jax.sharding import PartitionSpec as P

mix_rate = 0.5


def per_device(weight_up, low_up, high_up, norm_train, norm_step):
    fresh_up = weight_up.astype(jnp.float32) + mix_rate * jnp.dot(
        low_up, high_up, preferred_element_type=jnp.float32
    )
    total_up = lax.psum(jnp.sum(fresh_up * fresh_up, axis=0), "rows")
    scale_up = jnp.sqrt(total_up)
    narrow_up = (fresh_up / scale_up).astype(jnp.bfloat16)
    serve_up = lax.all_to_all(narrow_up, "rows", split_axis=1, concat_axis=0, tiled=True)
    place = lax.axis_index("rows")
    scale_up = lax.dynamic_slice_in_dim(scale_up, place * serve_up.shape[1], serve_up.shape[1])
    serve_norm = lax.all_gather(
        (norm_train + norm_step).astype(jnp.bfloat16), ("rows", "cols"), axis=0, tiled=True
    )
    return (serve_up, scale_up, serve_norm)


def solution(mesh):
    in_specs = (
        P("rows", "cols"),
        P("rows", None),
        P(None, "cols"),
        P(("rows", "cols")),
        P(("rows", "cols")),
    )
    out_specs = (P(None, ("cols", "rows")), P(("cols", "rows")), P())
    return jax.shard_map(
        per_device, mesh=mesh, in_specs=in_specs, out_specs=out_specs, check_vma=False
    )
```

profile of v0, /device:TPU:17, one launch (start us, length us, event | category | flops | bytes accessed | tf_op | source)
XLA Modules:
  0.0 1004.8 jit_solution(14810098583701876798)
XLA Ops:
  0.6 0.0 copy-start
  0.6 1.4 copy-done
  2.0 38.1 %multiply_reduce_fusion = (f32[12288]{0:T(1024)S(1)}, f32[1536,12288]{1,0:T(8,128)}) fusion(bf16[1536,64]{0,1:T(8,128)(2,1)} %param.6, bf16[64,12288]{1,0:T(8,128)(2,1)S(1)} %copy-done, bf16[1536,12288]{1,0:T(8,128)(2,1)} %param.5), kind=kOutput, calls=%fused_computation.1 | convolution fusion | flops 2510278656 | bytes 115064832 | tf_op jit(solution)/shard_map/dot_general | solution.py:10
  40.1 25.9 %psum.7 = f32[12288]{0:T(1024)S(1)} all-reduce(f32[12288]{0:T(1024)S(1)} %get-tuple-element.3), channel_id=1, replica_groups=mesh['rows'=8,'cols'=4] {'rows'}, use_global_device_ids=true, to_apply=%region_1.0 | all-reduce | flops 12288 | bytes 98304 | tf_op jit(solution)/shard_map/psum | solution.py:13
  66.0 36.5 %divide_convert_fusion = bf16[1536,12288]{1,0:T(8,128)(2,1)} fusion(f32[1536,12288]{1,0:T(8,128)} %get-tuple-element.4, f32[12288]{0:T(1024)S(1)} %sqrt.3), kind=kLoop, calls=%fused_computation | loop fusion | flops 37748736 | bytes 113295360 | tf_op jit(solution)/shard_map/convert_element_type | solution.py:15
  102.5 26.0 %copy.13 = bf16[192,8,8,1536]{3,2,0,1:T(8,128)(2,1)} copy(bf16[192,8,8,1536]{3,2,1,0:T(8,128)(2,1)} %bitcast.10) | data formatting | bytes 75497472 | tf_op jit(solution)/shard_map/all_to_all | solution.py:16
  128.5 0.0 copy-start.2
  128.5 0.0 copy-start.3
  128.5 12.3 %all-to-all-start = ((bf16[1536,8,1536]{2,0,1:T(8,128)(2,1)}), bf16[1536,8,1536]{2,0,1:T(8,128)(2,1)}, u32[]{:S(2)}, u32[]{:S(2)}) async-start(bf16[1536,8,1536]{2,0,1:T(8,128)(2,1)} %bitcast.9), calls=%async_computation | async-start | bytes 75497472 | tf_op jit(solution)/shard_map/all_to_all | solution.py:16
  140.8 0.7 dynamic_slice.3
  141.5 0.0 copy-done.2
  141.5 0.0 copy-done.3
  141.5 836.8 %all-gather = bf16[32,1,384]{2,1,0:T(2,128)(2,1)S(1)} all-gather(bf16[1,1,384]{2,1,0:T(2,128)(2,1)S(1)} %reshape.10), channel_id=1, replica_groups=mesh['rows'=8,'cols'=4] {'rows','cols'}, dimensions={0}, use_global_device_ids=true | all-gather | bytes 25344 | tf_op jit(solution)/shard_map/all_gather | solution.py:19
  978.3 0.1 reduce
  978.5 0.6 reshape.11
  979.1 0.0 all-to-all-done
  979.1 0.0 copy-start.1
  979.1 25.7 %copy.15 = bf16[12288,1536]{1,0:T(8,128)(2,1)} copy(bf16[12288,1536]{1,0:T(8,128)(2,1)} %bitcast.1) | data formatting | bytes 75497472
  1004.8 0.0 copy-done.1
  (3 shorter events, 0.0 us)
Async XLA Ops:
  0.6 1.4 copy-start
  128.5 13.0 %copy-start.2 = (f32[384]{0:T(512)S(1)}, f32[384]{0:T(512)}, u32[]{:S(2)}) copy-start(f32[384]{0:T(512)} %param.8) | copy-start | bytes 4612
  128.5 13.0 %copy-start.3 = (f32[384]{0:T(512)S(1)}, f32[384]{0:T(512)}, u32[]{:S(2)}) copy-start(f32[384]{0:T(512)} %param.9) | copy-start | bytes 4612
  128.5 850.6 %all-to-all-start = ((bf16[1536,8,1536]{2,0,1:T(8,128)(2,1)}), bf16[1536,8,1536]{2,0,1:T(8,128)(2,1)}, u32[]{:S(2)}, u32[]{:S(2)}) async-start(bf16[1536,8,1536]{2,0,1:T(8,128)(2,1)} %bitcast.9), calls=%async_computation | async-start | bytes 75497472 | tf_op jit(solution)/shard_map/all_to_all | solution.py:16
  979.1 25.8 %copy-start.1 = (bf16[64,12288]{1,0:T(8,128)(2,1)S(1)}, bf16[64,12288]{1,0:T(8,128)(2,1)}, u32[]{:S(2)}) copy-start(bf16[64,12288]{1,0:T(8,128)(2,1)} %param.7) | copy-start | bytes 4718596
where the time goes:
time: 1010 us; the launch traced here: 1000 us
  blocking collectives  863 us (85%)
  local copies, waits for them, and re-layouts  54.5 us (5%)
  matrix products  38.1 us (4%)
  other arithmetic  36.6 us (4%)
  starting transfers between devices  12.3 us (1%)
    all_gather x1, blocking collectives, per_device(): lax.all_gather((norm_train + norm_step).astype(jnp.bfloat16), ('rows', 'c...  837 us
    dot_general x1, matrix products, per_device(): jnp.dot(low_up, high_up, preferred_element_type=jnp.float32)  38.1 us
    convert_element_type x1, other arithmetic, per_device(): narrow_up = (fresh_up / scale_up).astype(jnp.bfloat16)  36.5 us
    unnamed x11, local copies, waits for them, and re-layouts  27.8 us
    all_to_all x1, local copies, waits for them, and re-layouts, per_device(): lax.all_to_all(narrow_up, 'rows', split_axis=1, concat_axis=0, tiled=True)  26 us
    psum x1, blocking collectives, per_device(): total_up = lax.psum(jnp.sum(fresh_up * fresh_up, axis=0), 'rows')  25.9 us
  transfers between devices with their start and end apart: 1, of which 0 were waited for; matrix products, arithmetic and copies ran while one was open for 0% of the time, Pallas kernels for 0%

commit v1 on v0

v1 whole, which is shorter than its diff:
```python
import functools
import math

import jax
import jax.numpy as jnp
from jax import lax
from jax.experimental import pallas as pl
from jax.experimental.pallas import tpu as pltpu
from jax.sharding import PartitionSpec as P


mix_rate = 0.5
lanes = 128
row_pack = 16


def chunk_widths(width):
    if width % lanes or width < 4 * lanes:
        return (width,)
    return (lanes, width - 2 * lanes, lanes)


def pack_kernel(weight_ref, *refs):
    chunk_ref = refs[-1]
    rows = weight_ref.shape[0]
    chunk_ref[0, :rows, :] = weight_ref[...]
    if len(refs) == 2:
        chunk_ref[0, rows:, :] = refs[0][...]


def pack(weight, rider, parts, start, part, width):
    rows = weight.shape[0]
    if part % lanes or width % lanes:
        chunk = jnp.transpose(
            weight.reshape(rows, parts, width)[:, :, start : start + part], (1, 0, 2)
        )
        if rider is not None:
            riders = jnp.broadcast_to(rider[None], (parts,) + rider.shape)
            chunk = jnp.concatenate([chunk, riders], axis=1)
        return chunk
    tile = math.gcd(math.gcd(width, start), part)
    tall = rows + (0 if rider is None else rider.shape[0])
    in_specs = [pl.BlockSpec((rows, tile), lambda d, j: (0, (d * width + start) // tile + j))]
    operands = [weight]
    if rider is not None:
        in_specs.append(pl.BlockSpec((rider.shape[0], tile), lambda d, j: (0, j)))
        operands.append(rider)
    return pl.pallas_call(
        pack_kernel,
        grid=(parts, part // tile),
        in_specs=in_specs,
        out_specs=pl.BlockSpec((1, tall, tile), lambda d, j: (d, 0, j)),
        out_shape=jax.ShapeDtypeStruct((parts, tall, part), weight.dtype),
        compiler_params=pltpu.CompilerParams(
            dimension_semantics=("arbitrary", "arbitrary"),
            vmem_limit_bytes=24 * 1024 * 1024,
        ),
        name="pack",
    )(*operands)


def normalise_kernel(rows, sub, w_ref, low_ref, high_ref, *refs):
    serve_ref, scale_ref, fresh_ref, sum_ref = refs[-4:]
    phase = pl.program_id(1)
    step = pl.program_id(2)
    group = w_ref.shape[0]
    width = w_ref.shape[2]
    fold = sum_ref.shape[0]
    streamed = low_ref.shape[0] < fresh_ref.shape[0]

    @pl.when(phase == 0)
    def _():
        @pl.when(step == 0)
        def _():
            sum_ref[...] = jnp.zeros_like(sum_ref)

        high = high_ref[...]

        def one(g, total):
            base = (step * group + g) * rows
            for s in range(0, rows, sub):
                at = pl.ds(pl.multiple_of(base + s, row_pack), sub)
                low = low_ref[pl.ds(pl.multiple_of(g * rows + s, row_pack), sub), :] if streamed else low_ref[at, :]
                mixed = jnp.dot(low, high, preferred_element_type=jnp.float32)
                fresh = w_ref[g, pl.ds(s, sub), :].astype(jnp.float32) + mixed
                fresh_ref[at, :] = fresh
                total = total + jnp.sum((fresh * fresh).reshape(sub // fold, fold, width), axis=0)
            return total

        sum_ref[...] = lax.fori_loop(0, group, one, sum_ref[...])

    @pl.when(phase == 1)
    def _():
        @pl.when(step == 0)
        def _():
            scale = jnp.sqrt(jnp.sum(sum_ref[...], axis=0, keepdims=True))
            scale_ref[...] = scale
            sum_ref[...] = jnp.broadcast_to(1.0 / scale, sum_ref.shape)

        inverse = sum_ref[0:1, :]

        def one(g, carry):
            base = g * rows
            for s in range(0, rows, sub):
                there = pl.ds(pl.multiple_of(base + s, row_pack), sub)
                here = pl.ds(pl.multiple_of(step * group * rows + base + s, row_pack), sub)
                serve_ref[there, :] = (fresh_ref[here, :] * inverse).astype(jnp.bfloat16)
            return carry

        lax.fori_loop(0, group, one, 0)


def normalise(arrived, low_all, high, serve, rows, start, serve_shape):
    parts, _, width = arrived.shape
    tile = next(t for t in (256, 128, width) if width % t == 0 and start % t == 0)
    base = start // tile
    whole = serve_shape[0]
    steps = 4 if parts % 4 == 0 else 1
    group = parts // steps
    sub = next(s for s in (256, 128, 64, 32, 16) if rows % s == 0)
    fold = 32 if sub % 32 == 0 else 8
    if width == tile:
        low_spec = pl.BlockSpec(
            (group * rows, low_all.shape[1]), lambda j, p, i: (jnp.where(p == 0, i, steps - 1), 0)
        )
    else:
        low_spec = pl.BlockSpec((whole, low_all.shape[1]), lambda j, p, i: (0, 0))
    in_specs = [
        pl.BlockSpec((group, rows, tile), lambda j, p, i: (jnp.where(p == 0, i, steps - 1), 0, j)),
        low_spec,
        pl.BlockSpec((high.shape[0], tile), lambda j, p, i: (0, j)),
    ]
    operands = [arrived, low_all, high]
    aliases = {}
    if serve is not None:
        in_specs.append(pl.BlockSpec(memory_space=pl.ANY))
        operands.append(serve)
        aliases = {3: 0}
    return pl.pallas_call(
        functools.partial(normalise_kernel, rows, sub),
        grid=(width // tile, 2, steps),
        in_specs=in_specs,
        out_specs=[
            pl.BlockSpec((group * rows, tile), lambda j, p, i: (jnp.where(p == 0, 0, i), base + j)),
            pl.BlockSpec((1, tile), lambda j, p, i: (0, j)),
        ],
        out_shape=[
            jax.ShapeDtypeStruct(serve_shape, jnp.bfloat16),
            jax.ShapeDtypeStruct((1, width), jnp.float32),
        ],
        scratch_shapes=[
            pltpu.VMEM((whole, tile), jnp.float32),
            pltpu.VMEM((fold, tile), jnp.float32),
        ],
        input_output_aliases=aliases,
        compiler_params=pltpu.CompilerParams(
            dimension_semantics=("arbitrary", "arbitrary", "arbitrary"),
            vmem_limit_bytes=48 * 1024 * 1024,
        ),
        name="normalise",
    )(*operands)


def per_device(n_rows, n_cols, weight_up, low_up, high_up, norm_train, norm_step):
    rows, span = weight_up.shape
    rank = low_up.shape[1]
    width = span // n_rows
    piece = rows // n_cols
    whole = rows * n_rows
    row_place = lax.axis_index("rows")
    col_place = lax.axis_index("cols")
    widths = chunk_widths(width)

    norm = (norm_train + norm_step).astype(jnp.bfloat16)
    low_turned = lax.dynamic_slice_in_dim(low_up.T, col_place * piece, piece, axis=1)
    rider = jnp.concatenate([low_turned, norm[None]], axis=0)
    held = rider.size
    unit = row_pack * widths[0]
    rider = jnp.pad(rider.reshape(-1), (0, -held % unit)).reshape(-1, widths[0])

    arrivals = []
    start = 0
    for index, part in enumerate(widths):
        chunk = pack(weight_up, None if index else rider, n_rows, start, part, width)
        arrived = lax.all_to_all(chunk, "rows", split_axis=0, concat_axis=0, tiled=True)
        arrivals.append(arrived)
        start += part

    mine = arrivals[0][:, rows:, :].reshape(n_rows, -1)[:, :held].reshape(n_rows, rank + 1, piece)
    spread = jnp.zeros((n_cols,) + mine.shape, mine.dtype)
    spread = lax.dynamic_update_index_in_dim(spread, mine, col_place, 0)
    for shift in range(1, n_cols):
        came = lax.ppermute(mine, "cols", [(c, (c + shift) % n_cols) for c in range(n_cols)])
        spread = lax.dynamic_update_index_in_dim(spread, came, (col_place - shift) % n_cols, 0)
    low_all = jnp.transpose(spread[:, :, :rank, :], (1, 0, 3, 2)).reshape(whole, rank)
    serve_norm = jnp.transpose(spread[:, :, rank, :], (1, 0, 2)).reshape(whole)

    high_own = mix_rate * lax.dynamic_slice_in_dim(high_up, row_place * width, width, axis=1)
    serve = None
    scales = []
    start = 0
    for part, arrived in zip(widths, arrivals):
        serve, scale = normalise(
            arrived, low_all, high_own[:, start : start + part], serve, rows, start, (whole, width)
        )
        scales.append(scale[0])
        start += part
    return (serve, jnp.concatenate(scales), serve_norm)


def in_layer(n_rows, n_cols, *args):
    return per_device(n_rows, n_cols, *args)


def solution(mesh):
    in_specs = (
        P("rows", "cols"),
        P("rows", None),
        P(None, "cols"),
        P(("rows", "cols")),
        P(("rows", "cols")),
    )
    out_specs = (P(None, ("cols", "rows")), P(("cols", "rows")), P())
    body = functools.partial(in_layer, mesh.shape["rows"], mesh.shape["cols"])
    return jax.shard_map(body, mesh=mesh, in_specs=in_specs, out_specs=out_specs, check_vma=False)
```

time: 1010 us -> 885 us (0.88)
  blocking collectives: 863 us -> 0 us
  waiting for transfers between devices: 0.01 us -> 710 us
  Pallas kernels: 0 us -> 130 us
  local copies, waits for them, and re-layouts: 54.5 us -> 11.1 us
  matrix products: 38.1 us -> 0 us
  other arithmetic: 36.6 us -> 2.33 us
  starting transfers between devices: 12.3 us -> 27.5 us
    all_gather x1 -> x0, blocking collectives: 837 us -> none  [per_device(): lax.all_gather((norm_train + norm_step).astype(jnp.bfloat16), ('rows', 'c...]
    all_to_all x1 -> x3, waiting for transfers between devices: 0.01 us -> 693 us  [per_device(): lax.all_to_all(chunk, 'rows', split_axis=0, concat_axis=0, tiled=True)]
    pallas_call x0 -> x6, Pallas kernels: none -> 130 us  [the longest x3 70.2 us: normalise(): pl.pallas_call(functools.partial(normalise_kernel, rows, sub), grid=(widt...]
    dot_general x1 -> x0, matrix products: 38.1 us -> none  [per_device(): jnp.dot(low_up, high_up, preferred_element_type=jnp.float32)]
    convert_element_type x2 -> x1, other arithmetic: 36.5 us -> 0.74 us  [per_device(): norm = (norm_train + norm_step).astype(jnp.bfloat16)]
    all_to_all x1 -> x0, local copies, waits for them, and re-layouts: 26 us -> none  [per_device(): lax.all_to_all(narrow_up, 'rows', split_axis=1, concat_axis=0, tiled=True)]
    psum x1 -> x0, blocking collectives: 25.9 us -> none  [per_device(): total_up = lax.psum(jnp.sum(fresh_up * fresh_up, axis=0), 'rows')]
    unnamed x11 -> x12, local copies, waits for them, and re-layouts: 27.8 us -> 4.26 us
  transfers between devices with their start and end apart: 1 -> 6, of which waited for: 0 -> 5; matrix products, arithmetic and copies ran while one was open for 0% -> 1% of each run, Pallas kernels for 0% -> 13%
where the time goes in v1:
time: 885 us; the launch traced here: 882 us
  waiting for transfers between devices  710 us (80%)
  Pallas kernels  130 us (15%)
  starting transfers between devices  27.5 us (3%)
  local copies, waits for them, and re-layouts  11.1 us (1%)
    all_to_all x3, waiting for transfers between devices, per_device(): lax.all_to_all(chunk, 'rows', split_axis=0, concat_axis=0, tiled=True)  693 us
    pallas_call x3, Pallas kernels, normalise(): pl.pallas_call(functools.partial(normalise_kernel, rows, sub), grid=(widt...  70.2 us
    pallas_call x3, Pallas kernels, pack(): pl.pallas_call(pack_kernel, grid=(parts, part // tile), in_specs=in_specs...  59.8 us
    all_to_all x3, starting transfers between devices, per_device(): lax.all_to_all(chunk, 'rows', split_axis=0, concat_axis=0, tiled=True)  24.1 us
  transfers between devices with their start and end apart: 6, of which 5 were waited for; matrix products, arithmetic and copies ran while one was open for 1% of the time, Pallas kernels for 13%

profile of v1, /device:TPU:17, one launch (start us, length us, event | category | flops | bytes accessed | tf_op | source)
XLA Modules:
  0.0 882.0 jit_solution(6935083784868662291)
XLA Ops:
  0.6 0.0 copy-start
  0.7 0.7 add_convert_fusion
  1.4 0.2 copy-done
  1.7 4.4 pack.4
  6.1 0.0 copy-start.3
  6.1 1.8 copy-done.3
  7.9 5.6 all-to-all-start.1
  13.5 49.2 %pack.5 = bf16[8,1536,1280]{2,1,0:T(8,128)(2,1)} custom-call(bf16[1536,12288]{1,0:T(8,128)(2,1)} %weight_ref.5), custom_call_target="tpu_custom_call" | custom-call | tf_op jit(solution)/shard_map/pack/pallas_call | solution.py:48
  62.7 26.8 %all-to-all-done.1.w_ref = bf16[8,1744,128]{2,1,0:T(8,128)(2,1)} async-done(((bf16[8,1744,128]{2,1,0:T(8,128)(2,1)}), bf16[8,1744,128]{2,1,0:T(8,128)(2,1)}, u32[]{:S(2)}, u32[]{:S(2)}) %all-to-all-start.1) | async-done | bytes 3571744 | tf_op jit(solution)/shard_map/all_to_all | solution.py:185
  89.5 9.9 %all-to-all-start.2 = ((bf16[8,1536,1280]{2,1,0:T(8,128)(2,1)}), bf16[8,1536,1280]{2,1,0:T(8,128)(2,1)}, u32[]{:S(2)}, u32[]{:S(2)}) async-start(bf16[8,1536,1280]{2,1,0:T(8,128)(2,1)} %pack.5), calls=%async_computation.2 | async-start | bytes 62914560 | tf_op jit(solution)/shard_map/all_to_all | solution.py:185
  99.4 6.2 pack.3
  105.6 666.6 %all-to-all-done.2.w_ref = bf16[8,1536,1280]{2,1,0:T(8,128)(2,1)} async-done(((bf16[8,1536,1280]{2,1,0:T(8,128)(2,1)}), bf16[8,1536,1280]{2,1,0:T(8,128)(2,1)}, u32[]{:S(2)}, u32[]{:S(2)}) %all-to-all-start.2) | async-done | bytes 31457312 | tf_op jit(solution)/shard_map/all_to_all | solution.py:185
  772.2 8.6 all-to-all-start
  780.8 1.0 slice_bitcast_fusion.1
  781.8 0.1 copy.25
  782.0 2.9 collective-permute-start
  784.8 1.0 dynamic-slice_multiply_fusion
  785.8 0.3 collective-permute-start.1
  786.1 0.2 collective-permute-start.2
  786.4 0.1 broadcast_in_dim.19
  786.5 0.1 constant_dynamic-update-slice_fusion
  786.6 5.7 collective-permute-done
  792.3 0.1 bitcast_dynamic-update-slice_fusion.2
  792.3 9.2 %collective-permute-done.1 = bf16[8,65,384]{2,0,1:T(8,128)(2,1)S(1)} collective-permute-done((bf16[8,65,384]{2,0,1:T(8,128)(2,1)S(1)}, bf16[8,65,384]{2,0,1:T(8,128)(2,1)S(1)}, u32[]{:S(2)}, u32[]{:S(2)}) %collective-permute-start.1) | collective-permute-done | bytes 399392 | tf_op jit(solution)/shard_map/ppermute | solution.py:193
  801.5 0.1 bitcast_dynamic-update-slice_fusion.1
  801.6 2.0 collective-permute-done.2
  803.5 0.1 bitcast_dynamic-update-slice_fusion
  803.6 0.0 copy-start.4
  803.6 1.1 copy-done.4
  804.8 1.3 slice_bitcast_fusion
  806.1 3.4 copy.21
  809.5 0.0 copy-start.2
  809.5 0.8 slice_bitcast_fusion.2
  810.3 0.8 reshape.30
  811.1 6.2 normalise.3
  817.3 0.0 copy-done.2
  817.3 57.3 %normalise.4 = (bf16[12288,1536]{1,0:T(8,128)(2,1)}, f32[1,1280]{1,0:T(1,128)S(1)}) custom-call(bf16[8,1536,1280]{2,1,0:T(8,128)(2,1)} %all-to-all-done.2.w_ref, bf16[12288,64]{1,0:T(8,128)(2,1)S(1)} %bitcast.35, bf16[64,1280]{1,0:T(8,128)(2,1)S(1)} %slice.32.high_ref, bf16[12288,1536]{1,0:T(8,128)(2,1)} %get-tuple-element.9.refs_0_), custom_call_target="tpu_custom_call", output_to_operand_aliasing={{0}: (3, {})} | custom-call | tf_op jit(solution)/shard_map/normalise/pallas_call | solution.py:139
  874.6 0.0 all-to-all-done.w_ref
  874.6 0.0 copy-start.1
  874.6 6.8 normalise.5
  881.4 0.6 pad_maximum_fusion.1
  882.0 0.0 copy-done.1
  (10 shorter events, 0.1 us)
Async XLA Ops:
  0.6 1.0 copy-start
  6.1 1.8 copy-start.3
  7.9 81.6 %all-to-all-start.1 = ((bf16[8,1744,128]{2,1,0:T(8,128)(2,1)}), bf16[8,1744,128]{2,1,0:T(8,128)(2,1)}, u32[]{:S(2)}, u32[]{:S(2)}) async-start(bf16[8,1744,128]{2,1,0:T(8,128)(2,1)} %copy-done.3), calls=%async_computation.1 | async-start | bytes 7143424 | tf_op jit(solution)/shard_map/all_to_all | solution.py:185
  89.5 682.7 %all-to-all-start.2 = ((bf16[8,1536,1280]{2,1,0:T(8,128)(2,1)}), bf16[8,1536,1280]{2,1,0:T(8,128)(2,1)}, u32[]{:S(2)}, u32[]{:S(2)}) async-start(bf16[8,1536,1280]{2,1,0:T(8,128)(2,1)} %pack.5), calls=%async_computation.2 | async-start | bytes 62914560 | tf_op jit(solution)/shard_map/all_to_all | solution.py:185
  772.2 102.4 %all-to-all-start = ((bf16[8,1536,128]{2,1,0:T(8,128)(2,1)}), bf16[8,1536,128]{2,1,0:T(8,128)(2,1)}, u32[]{:S(2)}, u32[]{:S(2)}) async-start(bf16[8,1536,128]{2,1,0:T(8,128)(2,1)} %pack.3), calls=%async_computation | async-start | bytes 6291456 | tf_op jit(solution)/shard_map/all_to_all | solution.py:185
  782.0 10.3 %collective-permute-start = (bf16[8,65,384]{2,0,1:T(8,128)(2,1)S(1)}, bf16[8,65,384]{2,0,1:T(8,128)(2,1)S(1)}, u32[]{:S(2)}, u32[]{:S(2)}) collective-permute-start(bf16[8,65,384]{2,0,1:T(8,128)(2,1)S(1)} %bitcast.40), channel_id=1, source_target_pairs={{0,1},{1,2},{2,3},{3,0},{4,5},{5,6},{6,7},{7,4},{8,9},{9,10},{10,1... | collective-permute-start | bytes 1198088 | tf_op jit(solution)/shard_map/ppermute | solution.py:193
  785.8 15.7 %collective-permute-start.1 = (bf16[8,65,384]{2,0,1:T(8,128)(2,1)S(1)}, bf16[8,65,384]{2,0,1:T(8,128)(2,1)S(1)}, u32[]{:S(2)}, u32[]{:S(2)}) collective-permute-start(bf16[8,65,384]{2,0,1:T(8,128)(2,1)S(1)} %bitcast.41), channel_id=1, source_target_pairs={{0,2},{1,3},{2,0},{3,1},{4,6},{5,7},{6,4},{7,5},{8,10},{9,11},{10,... | collective-permute-start | bytes 1198088 | tf_op jit(solution)/shard_map/ppermute | solution.py:193
  786.1 17.4 %collective-permute-start.2 = (bf16[8,65,384]{2,0,1:T(8,128)(2,1)S(1)}, bf16[8,65,384]{2,0,1:T(8,128)(2,1)S(1)}, u32[]{:S(2)}, u32[]{:S(2)}) collective-permute-start(bf16[8,65,384]{2,0,1:T(8,128)(2,1)S(1)} %bitcast.42), channel_id=1, source_target_pairs={{0,3},{1,0},{2,1},{3,2},{4,7},{5,4},{6,5},{7,6},{8,11},{9,8},{10,9... | collective-permute-start | bytes 1198088 | tf_op jit(solution)/shard_map/ppermute | solution.py:193
  803.6 1.2 copy-start.4
  809.5 7.8 copy-start.2
  874.6 7.4 copy-start.1
